TPU v7x, 256 devices: a whole 4x4x8 slice. The times are simulated.
256 devices in a mesh: section: 16 (over y, z_lo), dp: 16 (over z_hi, x, core).
Axes of the slice: x: 4, y: 4, z: 8 (z_hi: 2, z_lo: 4; z = z_hi * 4 + z_lo), core: 2. Of those that a mesh axis runs over, the one named last changes fastest.
Arguments:
- vit_weight: bfloat16 [16, 1280, 1280], P('section', 'dp'), may hold values from -0.078125 to 0.078125
- t5_weight: bfloat16 [16, 2048, 2048], P('section', 'dp'), may hold values from -0.0625 to 0.0625
- vit_saved: bfloat16 [16, 4, 512, 1280], P('section', None, 'dp'), may hold values from -6 to 6
- t5_saved: bfloat16 [16, 4, 512, 2048], P('section', None, 'dp'), may hold values from -6 to 6
- vit_top_grad: bfloat16 [4, 512, 1280], P(None, 'dp'), may hold values from -6 to 6
- t5_top_grad: bfloat16 [4, 512, 2048], P(None, 'dp'), may hold values from -6 to 6
Outputs:
- vit_input_grads: bfloat16 [16, 4, 512, 1280], P('section', None, 'dp')
- t5_input_grads: bfloat16 [16, 4, 512, 2048], P('section', None, 'dp')
- vit_weight_grads: float32 [16, 1280, 1280], P('section', 'dp')
- t5_weight_grads: float32 [16, 2048, 2048], P('section', 'dp')
All inputs are finite; a program needn't handle non-finite values.
Results may differ from a plain program's by a relative error of at most 0.02.
Values may be sent and summed in bfloat16 or wider, within the bound.
A program may use at most 128 MiB of HBM per device.

v0:
```python
import jax
import jax.numpy as jnp
from jax import lax
from jax.sharding import PartitionSpec as P

root_half = 0.7071067811865476
inv_root_tau = 0.3989422804014327


def in_order(parts, dim):
    shape = list(parts.shape[1:])
    shape[dim] *= parts.shape[0]
    return jnp.moveaxis(parts, 0, dim).reshape(shape)


def one_gather(arrays, axis, dims):
    flat = jnp.concatenate([a.reshape(-1) for a in arrays])
    lines, at, gathered = (lax.all_gather(flat, axis), 0, [])
    for a, dim in zip(arrays, dims):
        parts = lines[:, at : at + a.size].reshape(-1, *a.shape)
        gathered.append(in_order(parts, dim))
        at += a.size
    return tuple(gathered)


def shifted(block, axis, distance):
    devices = range(lax.axis_size(axis))
    route = [(i - distance, i) for i in devices if i - distance in devices]
    return lax.ppermute(block, axis, route)


def gelu_slope(preact):
    cumulative = 0.5 * (1.0 + lax.erf(preact * root_half))
    density = jnp.exp(-0.5 * preact * preact) * inv_root_tau
    return cumulative + preact * density


def layer_back(grad_above, saved_input, weight):
    preact = jnp.dot(saved_input, weight, preferred_element_type=jnp.float32)
    upper = grad_above.astype(jnp.float32)
    local_grad = (upper * gelu_slope(preact)).astype(jnp.bfloat16)
    through = lax.dot_general(
        local_grad, weight, (((1,), (1,)), ((), ())), preferred_element_type=jnp.float32
    )
    return ((upper + through).astype(jnp.bfloat16), local_grad)


def branch_tick(
    micro_index, received, top_grad, saved_all, weight, grad_buffer, local_buffer, is_last
):
    micro_count = saved_all.shape[0]
    active = jnp.logical_and(micro_index >= 0, micro_index < micro_count)
    micro_slot = jnp.clip(micro_index, 0, micro_count - 1)
    from_joining = lax.dynamic_index_in_dim(top_grad, micro_slot, 0, keepdims=False)
    incoming = jnp.where(is_last, from_joining, received)
    saved_input = lax.dynamic_index_in_dim(saved_all, micro_slot, 0, keepdims=False)

    def advance(operands):
        grad_above, layer_input, grads_now, locals_now = operands
        grad_below, local_grad = layer_back(grad_above, layer_input, weight)
        grads_now = lax.dynamic_update_index_in_dim(grads_now, grad_below, micro_slot, 0)
        locals_now = lax.dynamic_update_index_in_dim(locals_now, local_grad, micro_slot, 0)
        return (grad_below, grads_now, locals_now)

    def passed(operands):
        return (jnp.zeros_like(operands[0]), operands[2], operands[3])

    return lax.cond(active, advance, passed, (incoming, saved_input, grad_buffer, local_buffer))


def vit_weight_total(inputs, locals_all, token_scale):
    input_flat = inputs.reshape(-1, inputs.shape[2])
    local_flat = locals_all.reshape(-1, inputs.shape[2])
    return lax.psum_scatter(
        (
            lax.dot_general(
                input_flat, local_flat, (((0,), (0,)), ((), ())), preferred_element_type=jnp.float32
            )
            * token_scale
        ).astype(jnp.bfloat16),
        "dp",
        scatter_dimension=0,
        tiled=True,
    ).astype(jnp.float32)


def t5_weight_total(inputs, locals_all, token_scale):
    input_flat = inputs.reshape(-1, inputs.shape[2])
    local_flat = locals_all.reshape(-1, inputs.shape[2])
    return lax.psum_scatter(
        (
            lax.dot_general(
                input_flat, local_flat, (((0,), (0,)), ((), ())), preferred_element_type=jnp.float32
            )
            * token_scale
        ).astype(jnp.bfloat16),
        "dp",
        scatter_dimension=0,
        tiled=True,
    ).astype(jnp.float32)


def shards(vit_weight, t5_weight, vit_saved, t5_saved, vit_top_grad, t5_top_grad):
    section_count = lax.axis_size("section")
    section_index = lax.axis_index("section")
    is_last = section_index == section_count - 1
    vit_full, t5_full = one_gather((vit_weight[0], t5_weight[0]), "dp", (0, 0))
    vit_shape = vit_saved.shape[1:]
    token_scale = 1.0 / (vit_shape[0] * vit_shape[1])
    vit_inputs = vit_saved[0]
    t5_inputs = t5_saved[0]
    micro_count = vit_inputs.shape[0]
    depth = section_count - 1 - section_index
    vit_start = (
        jnp.zeros_like(vit_top_grad[0]),
        jnp.zeros_like(vit_inputs),
        jnp.zeros_like(vit_inputs),
    )
    t5_start = (
        jnp.zeros_like(t5_top_grad[0]),
        jnp.zeros_like(t5_inputs),
        jnp.zeros_like(t5_inputs),
    )

    def text_tick(tick_index, state_tuple):
        t5_recv, t5_grads, t5_locals = state_tuple
        t5_below, t5_grads, t5_locals = branch_tick(
            tick_index - depth,
            t5_recv,
            t5_top_grad,
            t5_inputs,
            t5_full,
            t5_grads,
            t5_locals,
            is_last,
        )
        t5_recv = shifted(t5_below, "section", -1)
        return (t5_recv, t5_grads, t5_locals)

    def image_tick(tick_index, state_tuple):
        vit_recv, vit_grads, vit_locals = state_tuple
        vit_below, vit_grads, vit_locals = branch_tick(
            tick_index - depth,
            vit_recv,
            vit_top_grad,
            vit_inputs,
            vit_full,
            vit_grads,
            vit_locals,
            is_last,
        )
        vit_recv = shifted(vit_below, "section", -1)
        return (vit_recv, vit_grads, vit_locals)

    text_state = lax.fori_loop(0, section_count + micro_count - 1, text_tick, t5_start)
    t5_grads, t5_locals = (text_state[1], text_state[2])
    t5_sum = t5_weight_total(t5_inputs, t5_locals, token_scale)
    image_state = lax.fori_loop(0, section_count + micro_count - 1, image_tick, vit_start)
    vit_grads, vit_locals = (image_state[1], image_state[2])
    vit_sum = vit_weight_total(vit_inputs, vit_locals, token_scale)
    return (vit_grads[None], t5_grads[None], vit_sum[None], t5_sum[None])


def solution(mesh):
    placed = (
        P("section", "dp", None),
        P("section", "dp", None),
        P("section", None, "dp", None),
        P("section", None, "dp", None),
        P(None, "dp", None),
        P(None, "dp", None),
    )
    return jax.shard_map(
        shards,
        mesh=mesh,
        in_specs=placed,
        out_specs=(
            P("section", None, "dp", None),
            P("section", None, "dp", None),
            P("section", "dp", None),
            P("section", "dp", None),
        ),
        check_vma=False,
    )
```

profile of v0, /device:TPU:1, one launch (start us, length us, event | category | flops | bytes accessed | tf_op | source)
XLA Modules:
  0.0 831.8 jit_solution(17774318324222367000)
XLA Ops:
  10.5 138.1 %all-gather.3.cloned.1.call-done = bf16[5832704]{0:T(1024)(128)(2,1)} async-done(((bf16[364544]{0:T(1024)(128)(2,1)}), bf16[5832704]{0:T(1024)(128)(2,1)}) %all-gather.3.cloned.1.call-update) | async-done | bytes 11665424 | tf_op jit(solution)/shard_map/all_gather | solution.py:18
  148.7 15.2 %reshape.18 = bf16[16,364544]{1,0:T(8,128)(2,1)} reshape(bf16[5832704]{0:T(1024)(128)(2,1)} %all-gather.3.cloned.1.call-done) | data formatting | bytes 23330816 | tf_op jit(solution)/shard_map/all_gather | solution.py:18
  163.9 3.9 slice.8
  167.8 2.9 reshape_reshape.6
  172.2 191.1 %while.34 = (s32[]{:T(128)}, bf16[32,1280]{1,0:T(8,128)(2,1)S(1)}, bf16[4,32,1280]{2,1,0:T(8,128)(2,1)}, bf16[4,32,1280]{2,1,0:T(8,128)(2,1)}, s32[]{:T(128)}, /...) while((s32[]{:T(128)}, bf16[32,1280]{1,0:T(8,128)(2,1)S(1)}, ...), condition=%wide.region_3.4_spmd, body=%wide.region_0.3_spmd.sunk | while | flops 210862080 | bytes 8032067 | solution.py:158
  173.6 4.3 collective-permute-done
  179.2 3.9 collective-permute-done
  184.4 3.9 collective-permute-done
  189.6 3.9 collective-permute-done
  194.9 5.8 collective-permute-done
  202.0 6.6 collective-permute-done
  209.9 6.6 collective-permute-done
  217.8 6.6 collective-permute-done
  225.7 6.9 collective-permute-done
  233.9 7.5 collective-permute-done
  242.8 7.1 collective-permute-done
  251.2 6.0 collective-permute-done
  258.5 6.3 collective-permute-done
  266.1 6.6 collective-permute-done
  274.1 39.4 %collective-permute-done = bf16[32,1280]{1,0:T(8,128)(2,1)S(1)} collective-permute-done((bf16[32,1280]{1,0:T(8,128)(2,1)S(1)}, bf16[32,1280]{1,0:T(8,128)(2,1)S(1)}, u32[]{:S(2)}, u32[]{:S(2)}) %collective-permute-start) | collective-permute-done | bytes 81952 | tf_op jit(solution)/shard_map/while/body/eval_jaxpr/ppermute | solution.py:29
  313.5 5.0 conditional.4
  319.7 7.3 collective-permute-done
  327.0 5.0 conditional.4
  329.3 2.7 bitcast_dynamic-update-slice_fusion
  333.3 7.5 collective-permute-done
  340.9 5.0 conditional.4
  343.1 2.7 bitcast_dynamic-update-slice_fusion
  347.1 6.0 collective-permute-done
  353.2 5.0 conditional.4
  359.4 3.9 collective-permute-done
  365.4 3.4 copy.14
  369.1 7.0 slice.9
  376.1 8.1 reshape_reshape.7
  384.3 251.5 %while.35 = (s32[]{:T(128)}, bf16[32,2048]{1,0:T(8,128)(2,1)S(1)}, bf16[4,32,2048]{2,1,0:T(8,128)(2,1)S(1)}, bf16[4,32,2048]{2,1,0:T(8,128)(2,1)S(1)}, s32[]{:T(...) while((s32[]{:T(128)}, bf16[32,2048]{1,0:T(8,128)(2,1)S(1)}, ...), condition=%wide.region_7.8_spmd, body=%wide.region_4.7_spmd.sunk | while | flops 538705920 | bytes 52694368 | solution.py:155
  385.7 4.4 collective-permute-done.1
  391.5 4.4 collective-permute-done.1
  397.2 4.4 collective-permute-done.1
  402.9 5.1 collective-permute-done.1
  409.4 6.1 collective-permute-done.1
  416.8 18.6 %collective-permute-done.1 = bf16[32,2048]{1,0:T(8,128)(2,1)S(1)} collective-permute-done((bf16[32,2048]{1,0:T(8,128)(2,1)S(1)}, bf16[32,2048]{1,0:T(8,128)(2,1)S(1)}, u32[]{:S(2)}, u32[]{:S(2)}) %collective-permute-start.1) | collective-permute-done | bytes 131104 | tf_op jit(solution)/shard_map/while/body/eval_jaxpr/ppermute | solution.py:29
  436.8 7.0 collective-permute-done.1
  445.1 5.9 collective-permute-done.1
  452.3 5.1 collective-permute-done.1
  458.8 12.0 %collective-permute-done.1 = bf16[32,2048]{1,0:T(8,128)(2,1)S(1)} collective-permute-done((bf16[32,2048]{1,0:T(8,128)(2,1)S(1)}, bf16[32,2048]{1,0:T(8,128)(2,1)S(1)}, u32[]{:S(2)}, u32[]{:S(2)}) %collective-permute-start.1) | collective-permute-done | bytes 131104 | tf_op jit(solution)/shard_map/while/body/eval_jaxpr/ppermute | solution.py:29
  472.1 4.8 collective-permute-done.1
  478.3 7.7 collective-permute-done.1
  487.3 6.3 collective-permute-done.1
  494.9 7.1 collective-permute-done.1
  503.4 66.5 %collective-permute-done.1 = bf16[32,2048]{1,0:T(8,128)(2,1)S(1)} collective-permute-done((bf16[32,2048]{1,0:T(8,128)(2,1)S(1)}, bf16[32,2048]{1,0:T(8,128)(2,1)S(1)}, u32[]{:S(2)}, u32[]{:S(2)}) %collective-permute-start.1) | collective-permute-done | bytes 131104 | tf_op jit(solution)/shard_map/while/body/eval_jaxpr/ppermute | solution.py:29
  569.9 8.3 %conditional.5 = (bf16[32,2048]{1,0:T(8,128)(2,1)S(1)}, bf16[4,32,2048]{2,1,0:T(8,128)(2,1)S(1)}, bf16[4,32,2048]{2,1,0:T(8,128)(2,1)S(1)}) conditional(s32[]{:T(128)} %convert_element_type.117, (bf16[4,32,2048]{2,1,0:T(8,128)(2,1)S(1)}, bf16[4,32,2048]{2,1,0:T(8,128)(2,1)S(1)}) %tuple.99, (pred[]{:T(512)}, s32[]{:T(128)}, ...), branch_computations={%region_5.5_spmd, %region_6.6_spmd} | conditional | flops 538705920 | bytes 52169804 | solution.py:68
  569.9 5.1 fusion.32
  579.6 7.1 collective-permute-done.1
  586.7 8.3 %conditional.5 = (bf16[32,2048]{1,0:T(8,128)(2,1)S(1)}, bf16[4,32,2048]{2,1,0:T(8,128)(2,1)S(1)}, bf16[4,32,2048]{2,1,0:T(8,128)(2,1)S(1)}) conditional(s32[]{:T(128)} %convert_element_type.117, (bf16[4,32,2048]{2,1,0:T(8,128)(2,1)S(1)}, bf16[4,32,2048]{2,1,0:T(8,128)(2,1)S(1)}) %tuple.99, (pred[]{:T(512)}, s32[]{:T(128)}, ...), branch_computations={%region_5.5_spmd, %region_6.6_spmd} | conditional | flops 538705920 | bytes 52169804 | solution.py:68
  586.7 5.1 fusion.32
  596.3 7.1 collective-permute-done.1
  603.4 8.3 %conditional.5 = (bf16[32,2048]{1,0:T(8,128)(2,1)S(1)}, bf16[4,32,2048]{2,1,0:T(8,128)(2,1)S(1)}, bf16[4,32,2048]{2,1,0:T(8,128)(2,1)S(1)}) conditional(s32[]{:T(128)} %convert_element_type.117, (bf16[4,32,2048]{2,1,0:T(8,128)(2,1)S(1)}, bf16[4,32,2048]{2,1,0:T(8,128)(2,1)S(1)}) %tuple.99, (pred[]{:T(512)}, s32[]{:T(128)}, ...), branch_computations={%region_5.5_spmd, %region_6.6_spmd} | conditional | flops 538705920 | bytes 52169804 | solution.py:68
  603.5 5.1 fusion.32
  613.1 7.1 collective-permute-done.1
  620.2 8.3 %conditional.5 = (bf16[32,2048]{1,0:T(8,128)(2,1)S(1)}, bf16[4,32,2048]{2,1,0:T(8,128)(2,1)S(1)}, bf16[4,32,2048]{2,1,0:T(8,128)(2,1)S(1)}) conditional(s32[]{:T(128)} %convert_element_type.117, (bf16[4,32,2048]{2,1,0:T(8,128)(2,1)S(1)}, bf16[4,32,2048]{2,1,0:T(8,128)(2,1)S(1)}) %tuple.99, (pred[]{:T(512)}, s32[]{:T(128)}, ...), branch_computations={%region_5.5_spmd, %region_6.6_spmd} | conditional | flops 538705920 | bytes 52169804 | solution.py:68
  620.2 5.1 fusion.32
  629.9 5.9 collective-permute-done.1
  635.8 5.6 fusion.50
  641.4 12.4 %copy.16 = bf16[2048,2048]{1,0:T(8,128)(2,1)} copy(bf16[2048,2048]{0,1:T(8,128)(2,1)} %fusion.50) | data formatting | bytes 16777216
  656.0 166.5 %reduce-scatter.9.cloned.1.call-done = bf16[128,2048]{1,0:T(8,128)(2,1)} async-done(((bf16[2048,2048]{1,0:T(8,128)(2,1)}), bf16[128,2048]{1,0:T(8,128)(2,1)}) %reduce-scatter.9.cloned.1.call-update) | async-done | bytes 524304
  (145 shorter events, 89.5 us)
Async XLA Ops:
  7.2 141.5 %all-gather.3.cloned.1.call-start = ((), (), s32[]{:S(2)}) async-start(), calls=%async_computation.2 | async-start | bytes 12394496 | tf_op jit(solution)/shard_map/all_gather | solution.py:18
  10.5 643.3 %reduce-scatter.7.cloned.1.call-start = ((), (), s32[]{:S(2)}) async-start(), calls=%async_computation.3 | async-start | bytes 3481600
  172.3 5.6 collective-permute-start
  177.9 5.2 collective-permute-start
  183.1 5.2 collective-permute-start
  188.3 5.2 collective-permute-start
  193.6 7.1 collective-permute-start
  200.7 7.9 collective-permute-start
  208.6 7.9 collective-permute-start
  216.5 7.9 collective-permute-start
  224.4 8.2 collective-permute-start
  232.6 8.8 %collective-permute-start = (bf16[32,1280]{1,0:T(8,128)(2,1)S(1)}, bf16[32,1280]{1,0:T(8,128)(2,1)S(1)}, u32[]{:S(2)}, u32[]{:S(2)}) collective-permute-start(bf16[32,1280]{1,0:T(8,128)(2,1)S(1)} %get-tuple-element.689), channel_id=1, source_target_pairs={{16,0},{32,16},{48,32},{64,48},{80,64},{96,80},{112,96},{128,112},... | collective-permute-start | bytes 245768 | tf_op jit(solution)/shard_map/while/body/eval_jaxpr/ppermute | solution.py:29
  241.4 8.4 %collective-permute-start = (bf16[32,1280]{1,0:T(8,128)(2,1)S(1)}, bf16[32,1280]{1,0:T(8,128)(2,1)S(1)}, u32[]{:S(2)}, u32[]{:S(2)}) collective-permute-start(bf16[32,1280]{1,0:T(8,128)(2,1)S(1)} %get-tuple-element.689), channel_id=1, source_target_pairs={{16,0},{32,16},{48,32},{64,48},{80,64},{96,80},{112,96},{128,112},... | collective-permute-start | bytes 245768 | tf_op jit(solution)/shard_map/while/body/eval_jaxpr/ppermute | solution.py:29
  249.9 7.3 collective-permute-start
  257.2 7.6 collective-permute-start
  264.8 7.9 collective-permute-start
  272.8 40.7 %collective-permute-start = (bf16[32,1280]{1,0:T(8,128)(2,1)S(1)}, bf16[32,1280]{1,0:T(8,128)(2,1)S(1)}, u32[]{:S(2)}, u32[]{:S(2)}) collective-permute-start(bf16[32,1280]{1,0:T(8,128)(2,1)S(1)} %get-tuple-element.689), channel_id=1, source_target_pairs={{16,0},{32,16},{48,32},{64,48},{80,64},{96,80},{112,96},{128,112},... | collective-permute-start | bytes 245768 | tf_op jit(solution)/shard_map/while/body/eval_jaxpr/ppermute | solution.py:29
  318.4 8.6 %collective-permute-start = (bf16[32,1280]{1,0:T(8,128)(2,1)S(1)}, bf16[32,1280]{1,0:T(8,128)(2,1)S(1)}, u32[]{:S(2)}, u32[]{:S(2)}) collective-permute-start(bf16[32,1280]{1,0:T(8,128)(2,1)S(1)} %get-tuple-element.689), channel_id=1, source_target_pairs={{16,0},{32,16},{48,32},{64,48},{80,64},{96,80},{112,96},{128,112},... | collective-permute-start | bytes 245768 | tf_op jit(solution)/shard_map/while/body/eval_jaxpr/ppermute | solution.py:29
  332.0 8.8 %collective-permute-start = (bf16[32,1280]{1,0:T(8,128)(2,1)S(1)}, bf16[32,1280]{1,0:T(8,128)(2,1)S(1)}, u32[]{:S(2)}, u32[]{:S(2)}) collective-permute-start(bf16[32,1280]{1,0:T(8,128)(2,1)S(1)} %get-tuple-element.689), channel_id=1, source_target_pairs={{16,0},{32,16},{48,32},{64,48},{80,64},{96,80},{112,96},{128,112},... | collective-permute-start | bytes 245768 | tf_op jit(solution)/shard_map/while/body/eval_jaxpr/ppermute | solution.py:29
  345.8 7.3 collective-permute-start
  358.1 5.2 collective-permute-start
  368.9 453.7 %reduce-scatter.9.cloned.1.call-start = ((), (), s32[]{:S(2)}) async-start(), calls=%async_computation.4 | async-start | bytes 8912896
  376.1 8.2 copy-start.1
  376.1 8.2 copy-start.2
  384.4 5.7 collective-permute-start.1
  390.2 5.7 collective-permute-start.1
  395.9 5.7 collective-permute-start.1
  401.6 6.4 collective-permute-start.1
  408.1 7.4 collective-permute-start.1
  415.5 19.9 %collective-permute-start.1 = (bf16[32,2048]{1,0:T(8,128)(2,1)S(1)}, bf16[32,2048]{1,0:T(8,128)(2,1)S(1)}, u32[]{:S(2)}, u32[]{:S(2)}) collective-permute-start(bf16[32,2048]{1,0:T(8,128)(2,1)S(1)} %get-tuple-element.701), channel_id=1, source_target_pairs={{16,0},{32,16},{48,32},{64,48},{80,64},{96,80},{112,96},{128,112},... | collective-permute-start | bytes 393224 | tf_op jit(solution)/shard_map/while/body/eval_jaxpr/ppermute | solution.py:29
  435.5 8.3 collective-permute-start.1
  443.8 7.2 collective-permute-start.1
  451.0 6.4 collective-permute-start.1
  457.5 13.3 %collective-permute-start.1 = (bf16[32,2048]{1,0:T(8,128)(2,1)S(1)}, bf16[32,2048]{1,0:T(8,128)(2,1)S(1)}, u32[]{:S(2)}, u32[]{:S(2)}) collective-permute-start(bf16[32,2048]{1,0:T(8,128)(2,1)S(1)} %get-tuple-element.701), channel_id=1, source_target_pairs={{16,0},{32,16},{48,32},{64,48},{80,64},{96,80},{112,96},{128,112},... | collective-permute-start | bytes 393224 | tf_op jit(solution)/shard_map/while/body/eval_jaxpr/ppermute | solution.py:29
  470.8 6.1 collective-permute-start.1
  477.0 9.0 %collective-permute-start.1 = (bf16[32,2048]{1,0:T(8,128)(2,1)S(1)}, bf16[32,2048]{1,0:T(8,128)(2,1)S(1)}, u32[]{:S(2)}, u32[]{:S(2)}) collective-permute-start(bf16[32,2048]{1,0:T(8,128)(2,1)S(1)} %get-tuple-element.701), channel_id=1, source_target_pairs={{16,0},{32,16},{48,32},{64,48},{80,64},{96,80},{112,96},{128,112},... | collective-permute-start | bytes 393224 | tf_op jit(solution)/shard_map/while/body/eval_jaxpr/ppermute | solution.py:29
  486.0 7.6 collective-permute-start.1
  493.6 8.4 %collective-permute-start.1 = (bf16[32,2048]{1,0:T(8,128)(2,1)S(1)}, bf16[32,2048]{1,0:T(8,128)(2,1)S(1)}, u32[]{:S(2)}, u32[]{:S(2)}) collective-permute-start(bf16[32,2048]{1,0:T(8,128)(2,1)S(1)} %get-tuple-element.701), channel_id=1, source_target_pairs={{16,0},{32,16},{48,32},{64,48},{80,64},{96,80},{112,96},{128,112},... | collective-permute-start | bytes 393224 | tf_op jit(solution)/shard_map/while/body/eval_jaxpr/ppermute | solution.py:29
  502.1 67.8 %collective-permute-start.1 = (bf16[32,2048]{1,0:T(8,128)(2,1)S(1)}, bf16[32,2048]{1,0:T(8,128)(2,1)S(1)}, u32[]{:S(2)}, u32[]{:S(2)}) collective-permute-start(bf16[32,2048]{1,0:T(8,128)(2,1)S(1)} %get-tuple-element.701), channel_id=1, source_target_pairs={{16,0},{32,16},{48,32},{64,48},{80,64},{96,80},{112,96},{128,112},... | collective-permute-start | bytes 393224 | tf_op jit(solution)/shard_map/while/body/eval_jaxpr/ppermute | solution.py:29
  569.9 5.8 copy-start
  578.3 8.4 %collective-permute-start.1 = (bf16[32,2048]{1,0:T(8,128)(2,1)S(1)}, bf16[32,2048]{1,0:T(8,128)(2,1)S(1)}, u32[]{:S(2)}, u32[]{:S(2)}) collective-permute-start(bf16[32,2048]{1,0:T(8,128)(2,1)S(1)} %get-tuple-element.701), channel_id=1, source_target_pairs={{16,0},{32,16},{48,32},{64,48},{80,64},{96,80},{112,96},{128,112},... | collective-permute-start | bytes 393224 | tf_op jit(solution)/shard_map/while/body/eval_jaxpr/ppermute | solution.py:29
  586.7 5.8 copy-start
  595.0 8.4 %collective-permute-start.1 = (bf16[32,2048]{1,0:T(8,128)(2,1)S(1)}, bf16[32,2048]{1,0:T(8,128)(2,1)S(1)}, u32[]{:S(2)}, u32[]{:S(2)}) collective-permute-start(bf16[32,2048]{1,0:T(8,128)(2,1)S(1)} %get-tuple-element.701), channel_id=1, source_target_pairs={{16,0},{32,16},{48,32},{64,48},{80,64},{96,80},{112,96},{128,112},... | collective-permute-start | bytes 393224 | tf_op jit(solution)/shard_map/while/body/eval_jaxpr/ppermute | solution.py:29
  603.4 5.8 copy-start
  611.8 8.4 %collective-permute-start.1 = (bf16[32,2048]{1,0:T(8,128)(2,1)S(1)}, bf16[32,2048]{1,0:T(8,128)(2,1)S(1)}, u32[]{:S(2)}, u32[]{:S(2)}) collective-permute-start(bf16[32,2048]{1,0:T(8,128)(2,1)S(1)} %get-tuple-element.701), channel_id=1, source_target_pairs={{16,0},{32,16},{48,32},{64,48},{80,64},{96,80},{112,96},{128,112},... | collective-permute-start | bytes 393224 | tf_op jit(solution)/shard_map/while/body/eval_jaxpr/ppermute | solution.py:29
  620.2 5.8 copy-start
  628.6 7.3 collective-permute-start.1
  635.8 18.0 %copy-start.3 = (bf16[4,32,2048]{2,1,0:T(8,128)(2,1)}, bf16[4,32,2048]{2,1,0:T(8,128)(2,1)S(1)}, u32[]{:S(2)}) copy-start(bf16[4,32,2048]{2,1,0:T(8,128)(2,1)S(1)} %get-tuple-element.527) | copy-start | bytes 1572868
Sparse Core Ops, SparseCore 0:
  11.3 137.3 all-gather.2
  369.0 109.5 reduce-scatter.6
  653.9 168.5 reduce-scatter.8
where the time goes:
time: 834 us; the launch traced here: 832 us
  waiting for transfers between devices  644 us (77%)
  local copies, waits for them, and re-layouts  64.4 us (8%)
  matrix products  58.5 us (7%)
  starting transfers between devices  49.4 us (6%)
  between operations  13.9 us (2%)
    ppermute x38, waiting for transfers between devices, shifted(): return lax.ppermute(block, axis, route)  339 us
    unnamed x5, waiting for transfers between devices  167 us
    all_gather x1, waiting for transfers between devices, one_gather(): lines, at, gathered = (lax.all_gather(flat, axis), 0, [])  138 us
    ppermute x38, starting transfers between devices, shifted(): return lax.ppermute(block, axis, route)  49.1 us
    dot_general x8, matrix products, layer_back(): preact = jnp.dot(saved_input, weight, preferred_element_type=jnp.float32)  29.7 us
    unnamed x13, local copies, waits for them, and re-layouts  21.7 us
    dot_general x8, matrix products, layer_back(): lax.dot_general(local_grad, weight, (((1,), (1,)), ((), ())), preferred_e...  21.1 us
  transfers between devices with their start and end apart: 41, of which 40 were waited for; matrix products, arithmetic and copies ran while one was open for 8% of the time, Pallas kernels for 0%

commit v1 on v0

v1 whole, which is shorter than its diff:
```python
import jax
import jax.numpy as jnp
from jax import lax
from jax.experimental import pallas as pl
from jax.experimental.pallas import tpu as pltpu
from jax.sharding import PartitionSpec as P

MESH = pl.DeviceIdType.MESH
root_half = 0.7071067811865476
inv_root_tau = 0.3989422804014327

SECTIONS = 16
DP = 16
DV = 1280
DT = 2048
RV = DV // DP
RT = DT // DP
TOK = 128
MICRO = 16
MB = TOK // MICRO
CHUNKS = 4
CT = 512
EARLY = 9


def slope_of(preact):
    cumulative = 0.5 * (1.0 + lax.erf(preact * root_half))
    density = jnp.exp(-0.5 * preact * preact) * inv_root_tau
    return cumulative + preact * density


def nt(a, b):
    return lax.dot_general(a, b, (((1,), (1,)), ((), ())), preferred_element_type=jnp.float32)


def nn(a, b):
    return jnp.dot(a, b, preferred_element_type=jnp.float32)


def ds(start, size, unit):
    return pl.ds(pl.multiple_of(start, unit), size)


class Gather:
    def __init__(self, slot, part, recv, pair, sent):
        self.slot, self.part, self.recv, self.pair, self.sent = slot, part, recv, pair, sent


def kernel(
    w5, wv, s5, sv, s5t, svt, top5, topv,
    g5o, gvo, d5o, dvo,
    W5, WV, L5, LV, S5, SV, G5, GV, P5, PV,
    rw5, rwv, rl5, rlv, pair, sent, c5, cv, csent, asem, asent, lsem,
):
    s = lax.axis_index("section")
    d = lax.axis_index("dp")
    zh = lax.div(d, 8)
    x = lax.rem(lax.div(d, 2), 4)
    c = lax.rem(d, 2)
    dr = 1 - 2 * c

    def dev(half, step, core):
        return lax.rem(zh + half, 2) * 8 + lax.rem(x + step + 8, 4) * 2 + core

    nx = dev(0, dr, c)
    zp = dev(1, 0, c)
    pt = dev(0, 0, 1 - c)
    first = s == SECTIONS - 1
    lower = s > 0
    early = s < EARLY

    barrier = pltpu.get_barrier_semaphore()

    def greet(p, _):
        pl.semaphore_signal(
            barrier, inc=1, device_id=(s, lax.rem(d + p, DP)), device_id_type=MESH
        )
        return 0

    lax.fori_loop(1, DP, greet, 0)

    @pl.when(lower)
    def _():
        pl.semaphore_signal(barrier, inc=1, device_id=(s - 1, d), device_id_type=MESH)

    @pl.when(s < SECTIONS - 1)
    def _():
        pl.semaphore_signal(barrier, inc=1, device_id=(s + 1, d), device_id_type=MESH)

    sections = lax.div(s + SECTIONS - 1, SECTIONS) + lax.div(2 * SECTIONS - 2 - s, SECTIONS)
    pl.semaphore_wait(barrier, DP - 1 + sections)

    gw5 = Gather(
        lambda v, q: W5.at[ds(q * (DT // CHUNKS), DT // CHUNKS, 16), ds(v * RT, RT, RT)],
        lambda n: W5.at[:, pl.ds(0, n * RT)],
        rw5, pair.at[0], sent.at[0],
    )
    gwv = Gather(
        lambda v, q: WV.at[ds(v * RV, RV, 16), :],
        lambda n: WV.at[pl.ds(0, n * RV), :],
        rwv, pair.at[1], sent.at[1],
    )
    gl5 = Gather(
        lambda v, q: L5.at[ds(v * TOK + q * (TOK // CHUNKS), TOK // CHUNKS, 16), :],
        lambda n: L5.at[pl.ds(0, n * TOK), :],
        rl5, pair.at[2], sent.at[2],
    )
    glv = Gather(
        lambda v, q: LV.at[ds(v * TOK + q * (TOK // CHUNKS), TOK // CHUNKS, 16), :],
        lambda n: LV.at[pl.ds(0, n * TOK), :],
        rlv, pair.at[3], sent.at[3],
    )

    def push(g, owner, q, recv, to):
        return pltpu.make_async_remote_copy(
            src_ref=g.slot(owner, q), dst_ref=g.slot(owner, q), send_sem=g.sent, recv_sem=recv,
            device_id=(s, to), device_id_type=MESH,
        )

    def own_ring(g, q):
        push(g, d, q, g.recv.at[0, 1, q], nx).start()

    def own_far(g, q):
        push(g, d, q, g.recv.at[1, 0, q], zp).start()

    def own_pair(g, q):
        push(g, d, q, g.pair, pt).start()

    def own(g, q):
        own_ring(g, q)
        own_far(g, q)
        own_pair(g, q)

    def forward(g, h, r, q):
        owner = dev(h, -r * dr, c)
        push(g, owner, q, g.recv.at[h, r, q], nx).wait_recv()
        if r < 3:
            push(g, owner, q, g.recv.at[h, r + 1, q], nx).start()
        push(g, owner, q, g.pair, pt).start()

    def forward_when(g, h, r, q):
        @pl.when(jnp.logical_and(q >= 0, q < CHUNKS))
        def _():
            forward(g, h, r, q)

    def ring_phase(g, r):
        def one(q, _):
            forward(g, 0, r, q)
            return 0

        lax.fori_loop(0, CHUNKS, one, 0)

    def far_phase(g):
        def one(w, _):
            for r in range(4):
                forward_when(g, 1, r, w - r)
            return 0

        lax.fori_loop(0, CHUNKS + 3, one, 0)

    def pair_done(g):
        ref = g.part(DP // 2)
        pltpu.make_async_copy(ref, ref, g.pair).wait()

    def sent_done(g):
        ref = g.part(DP - 1)
        pltpu.make_async_copy(ref, ref, g.sent).wait()

    own_w5 = pltpu.make_async_copy(w5, W5.at[:, ds(d * RT, RT, RT)], lsem.at[0])
    own_wv = pltpu.make_async_copy(wv, WV.at[ds(d * RV, RV, 16), :], lsem.at[1])
    own_s5 = pltpu.make_async_copy(
        s5t.at[ds(d * RT, RT, RT), :], S5.at[:, ds(d * TOK, TOK, TOK)], lsem.at[2]
    )
    own_sv = pltpu.make_async_copy(
        svt.at[ds(d * RV, RV, 16), :], SV.at[:, ds(d * TOK, TOK, TOK)], lsem.at[3]
    )
    own_w5.start()
    own_wv.start()
    own_s5.start()
    own_sv.start()
    own_w5.wait()
    for q in range(CHUNKS):
        own(gw5, q)
    own_wv.wait()
    own_far(gwv, 0)

    @pl.when(first)
    def _():
        a = pltpu.make_async_copy(top5, G5, lsem.at[0])
        b = pltpu.make_async_copy(topv, GV, lsem.at[1])
        a.start()
        b.start()
        a.wait()
        b.wait()

    own_s5.wait()
    own_sv.wait()
    for r in (1, 2, 3):
        ring_phase(gw5, r)
    far_phase(gw5)
    own_ring(gwv, 0)
    own_pair(gwv, 0)
    pair_done(gw5)

    def text_slope(j, _):
        cols = ds(j * CT, CT, CT)
        P5[:, cols] = slope_of(nt(s5[...], W5[cols, :]))
        return 0

    lax.fori_loop(0, DT // CT, text_slope, 0)

    image_steps = ((1, 0), (0, 1), (1, 1), (0, 2), (1, 2), (0, 3), (1, 3))

    def image_ready():
        pair_done(gwv)

        def one(j, _):
            cols = ds(j * 256, 256, 256)
            PV[:, cols] = slope_of(nn(sv[...], WV[:, cols]))
            return 0

        lax.fori_loop(0, DV // 256, one, 0)

        def send(p, _):
            t = lax.rem(d + p, DP)
            pltpu.make_async_remote_copy(
                src_ref=s5t.at[ds(t * RT, RT, RT), :], dst_ref=S5.at[:, ds(d * TOK, TOK, TOK)],
                send_sem=asent.at[0], recv_sem=asem.at[0], device_id=(s, t), device_id_type=MESH,
            ).start()
            pltpu.make_async_remote_copy(
                src_ref=svt.at[ds(t * RV, RV, 16), :], dst_ref=SV.at[:, ds(d * TOK, TOK, TOK)],
                send_sem=asent.at[1], recv_sem=asem.at[1], device_id=(s, t), device_id_type=MESH,
            ).start()
            return 0

        lax.fori_loop(1, DP, send, 0)

    @pl.when(early)
    def _():
        for h, r in image_steps:
            forward(gwv, h, r, 0)
        image_ready()

    def text_hop(k, n):
        rows, cols = ds(k * MICRO, MICRO, MICRO), pl.ds(n * CT, CT)
        return pltpu.make_async_remote_copy(
            src_ref=g5o.at[rows, cols], dst_ref=G5.at[rows, cols], send_sem=csent.at[0], recv_sem=c5.at[k, n],
            device_id=(s - 1, d), device_id_type=MESH,
        )

    def text_tick(k, _):
        rows = ds(k * MICRO, MICRO, MICRO)

        @pl.when(jnp.logical_not(first))
        def _():
            for n in range(DT // CT):
                text_hop(k, n).wait_recv()

        upper = G5[rows, :].astype(jnp.float32)
        local = (upper * P5[rows, :]).astype(jnp.bfloat16)
        L5[ds(d * TOK + k * MICRO, MICRO, MICRO), :] = local
        for n in range(DT // CT):
            cols = pl.ds(n * CT, CT)
            above = G5[rows, cols].astype(jnp.float32)
            g5o[rows, cols] = (above + nn(local, W5[:, cols])).astype(jnp.bfloat16)

            @pl.when(lower)
            def _():
                text_hop(k, n).start()

        odd = lax.rem(k, 2) == 1

        @pl.when(odd)
        def _():
            own(gl5, lax.div(k, 2))

        @pl.when(jnp.logical_and(odd, k >= 3))
        def _():
            forward(gl5, 0, 1, lax.div(k, 2) - 1)

        @pl.when(jnp.logical_not(early))
        def _():
            for i, (h, r) in enumerate(image_steps):

                @pl.when(k == i)
                def _():
                    forward(gwv, h, r, 0)

        return 0

    lax.fori_loop(0, MB, text_tick, 0)

    @pl.when(jnp.logical_not(early))
    def _():
        image_ready()

    def image_hop(k):
        rows = ds(k * MICRO, MICRO, MICRO)
        return pltpu.make_async_remote_copy(
            src_ref=gvo.at[rows, :], dst_ref=GV.at[rows, :], send_sem=csent.at[1], recv_sem=cv.at[k],
            device_id=(s - 1, d), device_id_type=MESH,
        )

    def image_tick(k, _):
        rows = ds(k * MICRO, MICRO, MICRO)

        @pl.when(jnp.logical_not(first))
        def _():
            image_hop(k).wait_recv()

        upper = GV[rows, :].astype(jnp.float32)
        local = (upper * PV[rows, :]).astype(jnp.bfloat16)
        LV[ds(d * TOK + k * MICRO, MICRO, MICRO), :] = local
        gvo[rows, :] = (upper + nt(local, WV[...])).astype(jnp.bfloat16)

        @pl.when(lower)
        def _():
            image_hop(k).start()

        @pl.when(lax.rem(k, 2) == 1)
        def _():
            own(glv, lax.div(k, 2))

        @pl.when(k == 0)
        def _():
            forward(gl5, 0, 1, CHUNKS - 1)

        forward_when(gl5, 0, 2, k)
        forward_when(gl5, 0, 3, k - 1)
        for r in range(4):
            forward_when(gl5, 1, r, k - 1 - r)
        return 0

    lax.fori_loop(0, MB, image_tick, 0)
    ring_phase(glv, 1)
    ring_phase(glv, 2)
    pair_done(gl5)
    got = S5.at[:, pl.ds(0, (DP - 1) * TOK)]
    pltpu.make_async_copy(got, got, asem.at[0]).wait()

    def text_total(j, _):
        cols = ds(j * CT, CT, CT)
        d5o[:, cols] = nn(S5[...], L5[:, cols]) * (1.0 / TOK)
        return 0

    lax.fori_loop(0, DT // CT, text_total, 0)
    ring_phase(glv, 3)
    far_phase(glv)
    pair_done(glv)
    got = SV.at[:, pl.ds(0, (DP - 1) * TOK)]
    pltpu.make_async_copy(got, got, asem.at[1]).wait()

    def image_total(j, _):
        cols = ds(j * 256, 256, 256)
        dvo[:, cols] = nn(SV[...], LV[:, cols]) * (1.0 / TOK)
        return 0

    lax.fori_loop(0, DV // 256, image_total, 0)
    for g in (gw5, gwv, gl5, glv):
        sent_done(g)
    gone = s5t.at[pl.ds(0, (DP - 1) * RT), :]
    pltpu.make_async_copy(gone, gone, asent.at[0]).wait()
    gone = svt.at[pl.ds(0, (DP - 1) * RV), :]
    pltpu.make_async_copy(gone, gone, asent.at[1]).wait()

    @pl.when(lower)
    def _():
        pltpu.make_async_copy(g5o, g5o, csent.at[0]).wait()
        pltpu.make_async_copy(gvo, gvo, csent.at[1]).wait()


def shards(vit_weight, t5_weight, vit_saved, t5_saved, vit_top_grad, t5_top_grad):
    s5 = t5_saved.reshape(TOK, DT)
    sv = vit_saved.reshape(TOK, DV)
    bf, f32 = jnp.bfloat16, jnp.float32
    dma, vmem = pltpu.SemaphoreType.DMA, pl.BlockSpec(memory_space=pltpu.VMEM)
    g5, gv, d5, dv = pl.pallas_call(
        kernel,
        out_shape=(
            jax.ShapeDtypeStruct((TOK, DT), bf),
            jax.ShapeDtypeStruct((TOK, DV), bf),
            jax.ShapeDtypeStruct((RT, DT), f32),
            jax.ShapeDtypeStruct((RV, DV), f32),
        ),
        in_specs=[vmem] * 8,
        out_specs=[vmem] * 4,
        scratch_shapes=[
            pltpu.VMEM((DT, DT), bf),
            pltpu.VMEM((DV, DV), bf),
            pltpu.VMEM((DP * TOK, DT), bf),
            pltpu.VMEM((DP * TOK, DV), bf),
            pltpu.VMEM((RT, DP * TOK), bf),
            pltpu.VMEM((RV, DP * TOK), bf),
            pltpu.VMEM((TOK, DT), bf),
            pltpu.VMEM((TOK, DV), bf),
            pltpu.VMEM((TOK, DT), f32),
            pltpu.VMEM((TOK, DV), f32),
            dma((2, 4, CHUNKS)),
            dma((2, 4, 1)),
            dma((2, 4, CHUNKS)),
            dma((2, 4, CHUNKS)),
            dma((4,)),
            dma((4,)),
            dma((MB, DT // CT)),
            dma((MB,)),
            dma((2,)),
            dma((2,)),
            dma((2,)),
            dma((4,)),
        ],
        compiler_params=pltpu.CompilerParams(
            collective_id=0, has_side_effects=True, vmem_limit_bytes=60 * 1024 * 1024
        ),
        name="branches",
    )(
        t5_weight[0].T,
        vit_weight[0],
        s5,
        sv,
        s5.T,
        sv.T,
        t5_top_grad.reshape(TOK, DT),
        vit_top_grad.reshape(TOK, DV),
    )
    return (
        gv.reshape(vit_saved.shape),
        g5.reshape(t5_saved.shape),
        dv[None],
        d5[None],
    )


def solution(mesh):
    placed = (
        P("section", "dp", None),
        P("section", "dp", None),
        P("section", None, "dp", None),
        P("section", None, "dp", None),
        P(None, "dp", None),
        P(None, "dp", None),
    )
    return jax.shard_map(
        shards,
        mesh=mesh,
        in_specs=placed,
        out_specs=(
            P("section", None, "dp", None),
            P("section", None, "dp", None),
            P("section", "dp", None),
            P("section", "dp", None),
        ),
        check_vma=False,
    )
```

time: 834 us -> 277 us (0.33)
  waiting for transfers between devices: 644 us -> 0 us
  Pallas kernels: 0 us -> 268 us
  matrix products: 58.5 us -> 0 us
  local copies, waits for them, and re-layouts: 64.4 us -> 8.29 us
  starting transfers between devices: 49.4 us -> 0 us
  between operations: 13.9 us -> 0.67 us
    ppermute x38 -> x0, waiting for transfers between devices: 339 us -> none  [shifted(): return lax.ppermute(block, axis, route)]
    pallas_call x0 -> x1, Pallas kernels: none -> 268 us  [shards(): pl.pallas_call(kernel, out_shape=(jax.ShapeDtypeStruct((TOK, DT), bf), ja...]
    unnamed x5 -> x0, waiting for transfers between devices: 167 us -> none
    all_gather x1 -> x0, waiting for transfers between devices: 138 us -> none  [one_gather(): lines, at, gathered = (lax.all_gather(flat, axis), 0, [])]
    dot_general x18 -> x0, matrix products: 58.5 us -> none  [the longest x8 29.7 us: layer_back(): preact = jnp.dot(saved_input, weight, preferred_element_type=jnp.float32)]
    ppermute x38 -> x0, starting transfers between devices: 49.1 us -> none  [shifted(): return lax.ppermute(block, axis, route)]
    unnamed x13 -> x15, local copies, waits for them, and re-layouts: 21.7 us -> 5.37 us
    all_gather x1 -> x0, local copies, waits for them, and re-layouts: 15.2 us -> none  [one_gather(): lines, at, gathered = (lax.all_gather(flat, axis), 0, [])]
  transfers between devices with their start and end apart: 41 -> 0, of which waited for: 40 -> 0; matrix products, arithmetic and copies ran while one was open for 8% -> 0% of each run, Pallas kernels for 0% -> 0%
where the time goes in v1:
time: 277 us
  Pallas kernels  268 us (97%)
  local copies, waits for them, and re-layouts  8.29 us (3%)
    pallas_call x1, Pallas kernels, shards(): pl.pallas_call(kernel, out_shape=(jax.ShapeDtypeStruct((TOK, DT), bf), ja...  268 us

profile of v1, /device:TPU:1, one launch (start us, length us, event | category | flops | bytes accessed | tf_op | source)
XLA Modules:
  0.0 277.3 jit_solution(10393043742409174978)
XLA Ops:
  0.6 0.0 copy-start.2
  0.6 1.9 copy.17
  2.6 0.0 copy-done.2
  2.6 0.0 copy-start
  2.6 1.0 copy.15
  3.6 0.0 copy-done
  3.6 1.0 copy.16
  4.6 268.3 %branches.1 = (bf16[128,2048]{1,0:T(8,128)(2,1)}, bf16[128,1280]{1,0:T(8,128)(2,1)}, f32[128,2048]{1,0:T(8,128)}, f32[80,1280]{1,0:T(8,128)}) custom-call(bf16[2048,128]{1,0:T(8,128)(2,1)} %bitcast.16, bf16[80,1280]{1,0:T(8,128)(2,1)} %bitcast.27, bf16[128,2048]{1,0:T(8,128)(2,1)} %bitcast.14, bf16[128,1280]{1,0:T(8,128)(2,1)} %bitcast.19, ...), custom_call_target="tpu_custom_call" | custom-call | tf_op jit(solution)/shard_map/branches/pallas_call | solution.py:377
  272.9 0.0 copy-start.3
  272.9 0.0 copy-start.4
  272.9 1.8 copy.22
  274.7 0.0 copy-done.3
  274.7 0.0 copy-start.1
  274.7 0.8 copy.23
  275.5 0.0 copy-done.4
  275.5 0.8 copy.24
  276.3 0.0 copy-done.1
  276.3 1.0 copy.25
Async XLA Ops:
  0.6 1.9 copy-start.2
  2.6 1.0 copy-start
  272.9 1.8 copy-start.3
  272.9 2.6 copy-start.4
  274.7 1.6 copy-start.1

commit v2 on v1

v2 whole, which is shorter than its diff:
```python
import jax
import jax.numpy as jnp
from jax import lax
from jax.experimental import pallas as pl
from jax.experimental.pallas import tpu as pltpu
from jax.sharding import PartitionSpec as P

MESH = pl.DeviceIdType.MESH
root_half = 0.7071067811865476
inv_root_tau = 0.3989422804014327

SECTIONS = 16
DP = 16
DV = 1280
DT = 2048
RV = DV // DP
RT = DT // DP
TOK = 128
MICRO = 16
MB = TOK // MICRO
HALF = DP // 2
PARTS = 2
CHUNKS = 4
CT = 512
EARLY = 9


def slope_of(preact):
    cumulative = 0.5 * (1.0 + lax.erf(preact * root_half))
    density = jnp.exp(-0.5 * preact * preact) * inv_root_tau
    return cumulative + preact * density


def nt(a, b):
    return lax.dot_general(a, b, (((1,), (1,)), ((), ())), preferred_element_type=jnp.float32)


def nn(a, b):
    return jnp.dot(a, b, preferred_element_type=jnp.float32)


def ds(start, size, unit):
    return pl.ds(pl.multiple_of(start, unit), size)


class Gather:
    def __init__(self, slot, part, recv, pair, sent, pieces, halves):
        self.slot, self.part, self.recv, self.pair, self.sent = slot, part, recv, pair, sent
        self.pieces, self.halves = pieces, halves


def kernel(
    w5, wv, s5, sv, top5, topv,
    g5o, gvo, d5o, dvo,
    W5, WV, L5, LV, S5, SV, G5, GV, P5, PV, s5t, svt, T5, TV, R5, RV2,
    rw5, rwv, rl5, rlv, pair, sent, c5, cv, csent, asem, asent, z5, zv, zsent, lsem,
):
    s = lax.axis_index("section")
    d = lax.axis_index("dp")
    zh = lax.div(d, 8)
    x = lax.rem(lax.div(d, 2), 4)
    c = lax.rem(d, 2)
    dr = 1 - 2 * c

    def dev(half, step, core):
        return lax.rem(zh + half, 2) * 8 + lax.rem(x + step + 8, 4) * 2 + core

    nx = dev(0, dr, c)
    zp = dev(1, 0, c)
    pt = dev(0, 0, 1 - c)
    first = s == SECTIONS - 1
    lower = s > 0
    early = s < EARLY
    u = lax.rem(d, HALF)

    barrier = pltpu.get_barrier_semaphore()

    def greet(p, _):
        pl.semaphore_signal(
            barrier, inc=1, device_id=(s, lax.rem(d + p, DP)), device_id_type=MESH
        )
        return 0

    lax.fori_loop(1, DP, greet, 0)

    @pl.when(lower)
    def _():
        pl.semaphore_signal(barrier, inc=1, device_id=(s - 1, d), device_id_type=MESH)

    @pl.when(s < SECTIONS - 1)
    def _():
        pl.semaphore_signal(barrier, inc=1, device_id=(s + 1, d), device_id_type=MESH)

    W5[:, ds(d * RT, RT, RT)] = w5[...].T
    s5t[...] = s5[...].T
    svt[...] = sv[...].T
    sections = lax.div(s + SECTIONS - 1, SECTIONS) + lax.div(2 * SECTIONS - 2 - s, SECTIONS)
    pl.semaphore_wait(barrier, DP - 1 + sections)

    gw5 = Gather(
        lambda v, q: W5.at[ds(q * (DT // PARTS), DT // PARTS, 16), ds(v * RT, RT, RT)],
        lambda n: W5.at[:, pl.ds(0, n * RT)],
        rw5, pair.at[0], sent.at[0], PARTS, 2,
    )
    gwv = Gather(
        lambda v, q: WV.at[ds(v * RV, RV, 16), :],
        lambda n: WV.at[pl.ds(0, n * RV), :],
        rwv, pair.at[1], sent.at[1], 1, 2,
    )
    piece = TOK // CHUNKS
    gl5 = Gather(
        lambda v, q: L5.at[ds(lax.rem(v, HALF) * TOK + q * piece, piece, 16), :],
        lambda n: L5.at[pl.ds(0, n * TOK), :],
        rl5, pair.at[2], sent.at[2], CHUNKS, 1,
    )
    glv = Gather(
        lambda v, q: LV.at[ds(lax.rem(v, HALF) * TOK + q * piece, piece, 16), :],
        lambda n: LV.at[pl.ds(0, n * TOK), :],
        rlv, pair.at[3], sent.at[3], CHUNKS, 1,
    )

    def push(g, owner, q, recv, to):
        return pltpu.make_async_remote_copy(
            src_ref=g.slot(owner, q), dst_ref=g.slot(owner, q), send_sem=g.sent, recv_sem=recv,
            device_id=(s, to), device_id_type=MESH,
        )

    def own_ring(g, q):
        push(g, d, q, g.recv.at[0, 1, q], nx).start()

    def own_far(g, q):
        push(g, d, q, g.recv.at[1, 0, q], zp).start()

    def own_pair(g, q):
        push(g, d, q, g.pair, pt).start()

    def own(g, q):
        own_ring(g, q)
        if g.halves == 2:
            own_far(g, q)
        own_pair(g, q)

    def forward(g, h, r, q):
        owner = dev(h, -r * dr, c)
        push(g, owner, q, g.recv.at[h, r, q], nx).wait_recv()
        if r < 3:
            push(g, owner, q, g.recv.at[h, r + 1, q], nx).start()
        push(g, owner, q, g.pair, pt).start()

    def forward_when(g, h, r, q):
        @pl.when(jnp.logical_and(q >= 0, q < g.pieces))
        def _():
            forward(g, h, r, q)

    def ring_phase(g, r):
        def one(q, _):
            forward(g, 0, r, q)
            return 0

        lax.fori_loop(0, g.pieces, one, 0)

    def far_phase(g):
        def one(w, _):
            for r in range(4):
                forward_when(g, 1, r, w - r)
            return 0

        lax.fori_loop(0, g.pieces + 3, one, 0)

    def pair_done(g):
        ref = g.part(4 * g.halves)
        pltpu.make_async_copy(ref, ref, g.pair).wait()

    def sent_done(g):
        ref = g.part(8 * g.halves - 1)
        pltpu.make_async_copy(ref, ref, g.sent).wait()

    own_wv = pltpu.make_async_copy(wv, WV.at[ds(d * RV, RV, 16), :], lsem.at[0])
    own_wv.start()
    for q in range(PARTS):
        own(gw5, q)
    own_wv.wait()
    own_far(gwv, 0)

    def saved_rows(h, v):
        text = s5t.at[ds(v * RT, RT, RT), :], S5.at[pl.ds(h * RT, RT), ds(u * TOK, TOK, TOK)]
        image = svt.at[ds(v * RV, RV, 16), :], SV.at[pl.ds(h * RV, RV), ds(u * TOK, TOK, TOK)]
        return text, image

    stay = []
    for h, v in ((0, d), (1, zp)):
        for i, (src, dst) in enumerate(saved_rows(h, v)):
            stay.append(pltpu.make_async_copy(src, dst, lsem.at[2 * h + i]))
    for copy in stay:
        copy.start()
    for copy in stay:
        copy.wait()

    @pl.when(first)
    def _():
        for k in range(MB):
            rows = pl.ds(k * MICRO, MICRO)
            for n in range(DT // CT):
                cols = pl.ds(n * CT, CT)
                pltpu.make_async_copy(top5.at[rows, cols], G5.at[rows, cols], c5.at[k, n]).start()
            pltpu.make_async_copy(topv.at[rows, :], GV.at[rows, :], cv.at[k]).start()

    for r in (1, 2, 3):
        ring_phase(gw5, r)
    far_phase(gw5)
    own_ring(gwv, 0)
    own_pair(gwv, 0)
    pair_done(gw5)

    def text_slope(j, _):
        cols = ds(j * CT, CT, CT)
        P5[:, cols] = slope_of(nt(s5[...], W5[cols, :]))
        return 0

    lax.fori_loop(0, DT // CT, text_slope, 0)

    image_steps = ((1, 0), (0, 1), (1, 1), (0, 2), (1, 2), (0, 3), (1, 3))

    def image_ready():
        pair_done(gwv)

        def one(j, _):
            cols = ds(j * 256, 256, 256)
            PV[:, cols] = slope_of(nn(sv[...], WV[:, cols]))
            return 0

        lax.fori_loop(0, DV // 256, one, 0)

        def send(p, _):
            up = lax.rem(u + p, HALF)
            t = zh * HALF + up
            for h, v in ((0, t), (1, (1 - zh) * HALF + up)):
                for i, (src, dst) in enumerate(saved_rows(h, v)):
                    pltpu.make_async_remote_copy(
                        src_ref=src, dst_ref=dst, send_sem=asent.at[i], recv_sem=asem.at[i],
                        device_id=(s, t), device_id_type=MESH,
                    ).start()
            return 0

        lax.fori_loop(1, HALF, send, 0)

    @pl.when(early)
    def _():
        for h, r in image_steps:
            forward(gwv, h, r, 0)
        image_ready()

    def text_hop(k, n):
        rows, cols = ds(k * MICRO, MICRO, MICRO), pl.ds(n * CT, CT)
        return pltpu.make_async_remote_copy(
            src_ref=g5o.at[rows, cols], dst_ref=G5.at[rows, cols], send_sem=csent.at[0], recv_sem=c5.at[k, n],
            device_id=(s - 1, d), device_id_type=MESH,
        )

    def text_tick(sends):
        def tick(k, _):
            rows = ds(k * MICRO, MICRO, MICRO)
            pieces = [pl.ds(n * CT, CT) for n in range(DT // CT)]
            total = [None] * len(pieces)
            for m, inner in enumerate(pieces):
                text_hop(k, m).wait_recv()
                local = (G5[rows, inner].astype(jnp.float32) * P5[rows, inner]).astype(jnp.bfloat16)
                L5[ds(u * TOK + k * MICRO, MICRO, MICRO), inner] = local
                for n, cols in enumerate(pieces):
                    term = nn(local, W5[inner, cols])
                    total[n] = term if m == 0 else total[n] + term
                    if m == len(pieces) - 1:
                        above = G5[rows, cols].astype(jnp.float32)
                        g5o[rows, cols] = (above + total[n]).astype(jnp.bfloat16)
                        if sends:
                            text_hop(k, n).start()

            @pl.when(jnp.logical_not(early))
            def _():
                for i, (h, r) in enumerate(image_steps):

                    @pl.when(k == i)
                    def _():
                        forward(gwv, h, r, 0)

            return 0

        lax.fori_loop(0, MB, tick, 0)

    @pl.when(lower)
    def _():
        text_tick(True)

    @pl.when(jnp.logical_not(lower))
    def _():
        text_tick(False)

    @pl.when(jnp.logical_not(early))
    def _():
        image_ready()

    def image_hop(k):
        rows = ds(k * MICRO, MICRO, MICRO)
        return pltpu.make_async_remote_copy(
            src_ref=gvo.at[rows, :], dst_ref=GV.at[rows, :], send_sem=csent.at[1], recv_sem=cv.at[k],
            device_id=(s - 1, d), device_id_type=MESH,
        )

    def exchange(out, got, recv, sem, n, width):
        cols = ds(n * width, width, width)
        return pltpu.make_async_remote_copy(
            src_ref=out.at[:, cols], dst_ref=got.at[:, cols], send_sem=zsent.at[sem], recv_sem=recv.at[n],
            device_id=(s, zp), device_id_type=MESH,
        )

    def far_rows(saved, local, rows, out, got, recv, sem, width):
        def one(n, _):
            cols = ds(n * width, width, width)
            term = nn(saved[pl.ds(rows, rows), :], local[:, cols]) * (1.0 / TOK)
            out[:, cols] = term.astype(jnp.bfloat16)
            exchange(out, got, recv, sem, n, width).start()
            return 0

        lax.fori_loop(0, local.shape[1] // width, one, 0)

    def near_rows(saved, local, rows, total, width):
        def one(n, _):
            cols = ds(n * width, width, width)
            total[:, cols] = nn(saved[pl.ds(0, rows), :], local[:, cols]) * (1.0 / TOK)
            return 0

        lax.fori_loop(0, local.shape[1] // width, one, 0)

    def add_far(total, out, got, recv, sem, width):
        def one(n, _):
            cols = ds(n * width, width, width)
            exchange(out, got, recv, sem, n, width).wait_recv()
            total[:, cols] += got[:, cols].astype(jnp.float32)
            return 0

        lax.fori_loop(0, total.shape[1] // width, one, 0)

    def saved_done(ref, i):
        got = ref.at[:, pl.ds(0, (HALF - 1) * TOK)]
        pltpu.make_async_copy(got, got, asem.at[i]).wait()

    def image_tick(k, _):
        rows = ds(k * MICRO, MICRO, MICRO)
        image_hop(k).wait_recv()
        upper = GV[rows, :].astype(jnp.float32)
        local = (upper * PV[rows, :]).astype(jnp.bfloat16)
        LV[ds(u * TOK + k * MICRO, MICRO, MICRO), :] = local
        gvo[rows, :] = (upper + nt(local, WV[...])).astype(jnp.bfloat16)

        @pl.when(lower)
        def _():
            image_hop(k).start()

        return 0

    lax.fori_loop(0, MB, image_tick, 0)
    def own_all(g):
        def one(q, _):
            own(g, q)
            return 0

        lax.fori_loop(0, g.pieces, one, 0)

    own_all(gl5)
    ring_phase(gl5, 1)
    ring_phase(gl5, 2)
    own_all(glv)
    ring_phase(gl5, 3)
    pair_done(gl5)
    saved_done(S5, 0)
    far_rows(S5, L5, RT, T5, R5, z5, 0, CT)
    ring_phase(glv, 1)
    ring_phase(glv, 2)
    near_rows(S5, L5, RT, d5o, CT)
    ring_phase(glv, 3)
    pair_done(glv)
    saved_done(SV, 1)
    far_rows(SV, LV, RV, TV, RV2, zv, 1, 256)
    near_rows(SV, LV, RV, dvo, 256)
    add_far(d5o, T5, R5, z5, 0, CT)
    add_far(dvo, TV, RV2, zv, 1, 256)
    for g in (gw5, gwv, gl5, glv):
        sent_done(g)
    for i, (ref, size) in enumerate(((s5t, RT), (svt, RV))):
        gone = ref.at[pl.ds(0, 2 * (HALF - 1) * size), :]
        pltpu.make_async_copy(gone, gone, asent.at[i]).wait()
    pltpu.make_async_copy(T5, T5, zsent.at[0]).wait()
    pltpu.make_async_copy(TV, TV, zsent.at[1]).wait()

    @pl.when(lower)
    def _():
        pltpu.make_async_copy(g5o, g5o, csent.at[0]).wait()
        pltpu.make_async_copy(gvo, gvo, csent.at[1]).wait()


def shards(vit_weight, t5_weight, vit_saved, t5_saved, vit_top_grad, t5_top_grad):
    bf, f32 = jnp.bfloat16, jnp.float32
    dma, vmem = pltpu.SemaphoreType.DMA, pl.BlockSpec(memory_space=pltpu.VMEM)
    g5, gv, d5, dv = pl.pallas_call(
        kernel,
        out_shape=(
            jax.ShapeDtypeStruct((TOK, DT), bf),
            jax.ShapeDtypeStruct((TOK, DV), bf),
            jax.ShapeDtypeStruct((RT, DT), f32),
            jax.ShapeDtypeStruct((RV, DV), f32),
        ),
        in_specs=[vmem] * 6,
        out_specs=[vmem] * 4,
        scratch_shapes=[
            pltpu.VMEM((DT, DT), bf),
            pltpu.VMEM((DV, DV), bf),
            pltpu.VMEM((HALF * TOK, DT), bf),
            pltpu.VMEM((HALF * TOK, DV), bf),
            pltpu.VMEM((2 * RT, HALF * TOK), bf),
            pltpu.VMEM((2 * RV, HALF * TOK), bf),
            pltpu.VMEM((TOK, DT), bf),
            pltpu.VMEM((TOK, DV), bf),
            pltpu.VMEM((TOK, DT), f32),
            pltpu.VMEM((TOK, DV), f32),
            pltpu.VMEM((DT, TOK), bf),
            pltpu.VMEM((DV, TOK), bf),
            pltpu.VMEM((RT, DT), bf),
            pltpu.VMEM((RV, DV), bf),
            pltpu.VMEM((RT, DT), bf),
            pltpu.VMEM((RV, DV), bf),
            dma((2, 4, PARTS)),
            dma((2, 4, 1)),
            dma((1, 4, CHUNKS)),
            dma((1, 4, CHUNKS)),
            dma((4,)),
            dma((4,)),
            dma((MB, DT // CT)),
            dma((MB,)),
            dma((2,)),
            dma((2,)),
            dma((2,)),
            dma((DT // CT,)),
            dma((DV // 256,)),
            dma((2,)),
            dma((4,)),
        ],
        compiler_params=pltpu.CompilerParams(
            collective_id=0, has_side_effects=True, vmem_limit_bytes=60 * 1024 * 1024
        ),
        name="branches",
    )(
        t5_weight[0],
        vit_weight[0],
        t5_saved.reshape(TOK, DT),
        vit_saved.reshape(TOK, DV),
        t5_top_grad.reshape(TOK, DT),
        vit_top_grad.reshape(TOK, DV),
    )
    return (
        gv.reshape(vit_saved.shape),
        g5.reshape(t5_saved.shape),
        dv[None],
        d5[None],
    )


def solution(mesh):
    placed = (
        P("section", "dp", None),
        P("section", "dp", None),
        P("section", None, "dp", None),
        P("section", None, "dp", None),
        P(None, "dp", None),
        P(None, "dp", None),
    )
    return jax.shard_map(
        shards,
        mesh=mesh,
        in_specs=placed,
        out_specs=(
            P("section", None, "dp", None),
            P("section", None, "dp", None),
            P("section", "dp", None),
            P("section", "dp", None),
        ),
        check_vma=False,
    )
```

time: 277 us -> 210 us (0.76)
  Pallas kernels: 268 us -> 205 us
  local copies, waits for them, and re-layouts: 8.29 us -> 4.32 us
    pallas_call x1, Pallas kernels: 268 us -> 205 us  [shards(): pl.pallas_call(kernel, out_shape=(jax.ShapeDtypeStruct((TOK, DT), bf), ja...]
    reshape x2 -> x0, local copies, waits for them, and re-layouts: 2.93 us -> none  [the longest x1 1.93 us: shards(): sv = vit_saved.reshape(TOK, DV)]
where the time goes in v2:
time: 210 us
  Pallas kernels  205 us (98%)
  local copies, waits for them, and re-layouts  4.32 us (2%)
    pallas_call x1, Pallas kernels, shards(): pl.pallas_call(kernel, out_shape=(jax.ShapeDtypeStruct((TOK, DT), bf), ja...  205 us
    unnamed x10, local copies, waits for them, and re-layouts  4.32 us

profile of v2, /device:TPU:1, one launch (start us, length us, event | category | flops | bytes accessed | tf_op | source)
XLA Modules:
  0.0 209.7 jit_solution(13446333469922375099)
XLA Ops:
  0.6 204.7 %branches.1 = (bf16[128,2048]{1,0:T(8,128)(2,1)}, bf16[128,1280]{1,0:T(8,128)(2,1)}, f32[128,2048]{1,0:T(8,128)}, f32[80,1280]{1,0:T(8,128)}) custom-call(bf16[128,2048]{1,0:T(8,128)(2,1)} %bitcast.11, bf16[80,1280]{1,0:T(8,128)(2,1)} %bitcast.19, bf16[128,2048]{1,0:T(8,128)(2,1)} %bitcast.12, bf16[128,1280]{1,0:T(8,128)(2,1)} %bitcast.16, ...), custom_call_target="tpu_custom_call" | custom-call | tf_op jit(solution)/shard_map/branches/pallas_call | solution.py:404
  205.3 0.0 copy-start.1
  205.4 0.0 copy-start.2
  205.4 1.8 copy.14
  207.2 0.0 copy-done.1
  207.2 0.0 copy-start
  207.2 0.8 copy.15
  208.0 0.0 copy-done.2
  208.0 0.8 copy.16
  208.7 0.0 copy-done
  208.7 1.0 copy.17
Async XLA Ops:
  205.3 1.8 copy-start.1
  205.4 2.6 %copy-start.2 = (f32[80,1280]{1,0:T(8,128)S(1)}, f32[80,1280]{1,0:T(8,128)}, u32[]{:S(2)}) copy-start(f32[80,1280]{1,0:T(8,128)} %get-tuple-element.10) | copy-start | bytes 1228804
  207.2 1.6 copy-start

commit v3 on v2

--- a/solution.py
+++ b/solution.py
@@ -20,7 +20,8 @@
 MB = TOK // MICRO
 HALF = DP // 2
 PARTS = 2
-CHUNKS = 4
+CHUNKS = 8
+CHUNKS_V = 2
 CT = 512
 EARLY = 9
 
@@ -52,7 +53,7 @@
 def kernel(
     w5, wv, s5, sv, top5, topv,
     g5o, gvo, d5o, dvo,
-    W5, WV, L5, LV, S5, SV, G5, GV, P5, PV, s5t, svt, T5, TV, R5, RV2,
+    W5, WV, L5, LV, S5, SV, G5, GV, P5, PV, s5t, svt, T5, TV, R5, RV2, WT,
     rw5, rwv, rl5, rlv, pair, sent, c5, cv, csent, asem, asent, z5, zv, zsent, lsem,
 ):
     s = lax.axis_index("section")
@@ -92,8 +93,6 @@
         pl.semaphore_signal(barrier, inc=1, device_id=(s + 1, d), device_id_type=MESH)
 
     W5[:, ds(d * RT, RT, RT)] = w5[...].T
-    s5t[...] = s5[...].T
-    svt[...] = sv[...].T
     sections = lax.div(s + SECTIONS - 1, SECTIONS) + lax.div(2 * SECTIONS - 2 - s, SECTIONS)
     pl.semaphore_wait(barrier, DP - 1 + sections)
 
@@ -114,9 +113,9 @@
         rl5, pair.at[2], sent.at[2], CHUNKS, 1,
     )
     glv = Gather(
-        lambda v, q: LV.at[ds(lax.rem(v, HALF) * TOK + q * piece, piece, 16), :],
+        lambda v, q: LV.at[ds(lax.rem(v, HALF) * TOK + q * (TOK // CHUNKS_V), TOK // CHUNKS_V, 16), :],
         lambda n: LV.at[pl.ds(0, n * TOK), :],
-        rlv, pair.at[3], sent.at[3], CHUNKS, 1,
+        rlv, pair.at[3], sent.at[3], CHUNKS_V, 1,
     )
 
     def push(g, owner, q, recv, to):
@@ -181,6 +180,8 @@
         own(gw5, q)
     own_wv.wait()
     own_far(gwv, 0)
+    s5t[...] = s5[...].T
+    svt[...] = sv[...].T
 
     def saved_rows(h, v):
         text = s5t.at[ds(v * RT, RT, RT), :], S5.at[pl.ds(h * RT, RT), ds(u * TOK, TOK, TOK)]
@@ -223,6 +224,7 @@
 
     def image_ready():
         pair_done(gwv)
+        WT[...] = WV[...].T
 
         def one(j, _):
             cols = ds(j * 256, 256, 256)
@@ -275,6 +277,8 @@
                         if sends:
                             text_hop(k, n).start()
 
+            own(gl5, k)
+
             @pl.when(jnp.logical_not(early))
             def _():
                 for i, (h, r) in enumerate(image_steps):
@@ -350,11 +354,13 @@
         upper = GV[rows, :].astype(jnp.float32)
         local = (upper * PV[rows, :]).astype(jnp.bfloat16)
         LV[ds(u * TOK + k * MICRO, MICRO, MICRO), :] = local
-        gvo[rows, :] = (upper + nt(local, WV[...])).astype(jnp.bfloat16)
+        gvo[rows, :] = (upper + nn(local, WT[...])).astype(jnp.bfloat16)
 
         @pl.when(lower)
         def _():
             image_hop(k).start()
+
+        forward(gl5, 0, 1, k)
 
         return 0
 
@@ -366,8 +372,6 @@
 
         lax.fori_loop(0, g.pieces, one, 0)
 
-    own_all(gl5)
-    ring_phase(gl5, 1)
     ring_phase(gl5, 2)
     own_all(glv)
     ring_phase(gl5, 3)
@@ -428,10 +432,11 @@
             pltpu.VMEM((RV, DV), bf),
             pltpu.VMEM((RT, DT), bf),
             pltpu.VMEM((RV, DV), bf),
+            pltpu.VMEM((DV, DV), bf),
             dma((2, 4, PARTS)),
             dma((2, 4, 1)),
             dma((1, 4, CHUNKS)),
-            dma((1, 4, CHUNKS)),
+            dma((1, 4, CHUNKS_V)),
             dma((4,)),
             dma((4,)),
             dma((MB, DT // CT)),

time: 210 us -> 198 us (0.943)
  Pallas kernels: 205 us -> 193 us
    pallas_call x1, Pallas kernels: 205 us -> 193 us  [shards(): pl.pallas_call(kernel, out_shape=(jax.ShapeDtypeStruct((TOK, DT), bf), ja...]
where the time goes in v3:
time: 198 us
  Pallas kernels  193 us (97%)
  local copies, waits for them, and re-layouts  4.32 us (2%)
    pallas_call x1, Pallas kernels, shards(): pl.pallas_call(kernel, out_shape=(jax.ShapeDtypeStruct((TOK, DT), bf), ja...  193 us
    unnamed x10, local copies, waits for them, and re-layouts  4.32 us

profile of v3, /device:TPU:1, one launch (start us, length us, event | category | flops | bytes accessed | tf_op | source)
XLA Modules:
  0.0 198.1 jit_solution(16264895907471840205)
XLA Ops:
  0.6 193.1 %branches.1 = (bf16[128,2048]{1,0:T(8,128)(2,1)}, bf16[128,1280]{1,0:T(8,128)(2,1)}, f32[128,2048]{1,0:T(8,128)}, f32[80,1280]{1,0:T(8,128)}) custom-call(bf16[128,2048]{1,0:T(8,128)(2,1)} %bitcast.11, bf16[80,1280]{1,0:T(8,128)(2,1)} %bitcast.19, bf16[128,2048]{1,0:T(8,128)(2,1)} %bitcast.12, bf16[128,1280]{1,0:T(8,128)(2,1)} %bitcast.16, ...), custom_call_target="tpu_custom_call" | custom-call | tf_op jit(solution)/shard_map/branches/pallas_call | solution.py:408
  193.7 0.0 copy-start.1
  193.7 0.0 copy-start.2
  193.7 1.8 copy.14
  195.5 0.0 copy-done.1
  195.5 0.0 copy-start
  195.5 0.8 copy.15
  196.3 0.0 copy-done.2
  196.3 0.8 copy.16
  197.1 0.0 copy-done
  197.1 1.0 copy.17
Async XLA Ops:
  193.7 1.8 copy-start.1
  193.7 2.6 %copy-start.2 = (f32[80,1280]{1,0:T(8,128)S(1)}, f32[80,1280]{1,0:T(8,128)}, u32[]{:S(2)}) copy-start(f32[80,1280]{1,0:T(8,128)} %get-tuple-element.10) | copy-start | bytes 1228804
  195.5 1.6 copy-start

commit v4 on v3

--- a/solution.py
+++ b/solution.py
@@ -23,6 +23,12 @@
 CHUNKS = 8
 CHUNKS_V = 2
 CT = 512
+RELAYED = 2
+ROW = 4
+RELAY = SECTIONS - ROW
+KEPT = (2, 3)
+EAGER = 2
+LAG = 3
 EARLY = 9
 
 
@@ -53,8 +59,8 @@
 def kernel(
     w5, wv, s5, sv, top5, topv,
     g5o, gvo, d5o, dvo,
-    W5, WV, L5, LV, S5, SV, G5, GV, P5, PV, s5t, svt, T5, TV, R5, RV2, WT,
-    rw5, rwv, rl5, rlv, pair, sent, c5, cv, csent, asem, asent, z5, zv, zsent, lsem,
+    W5, WV, L5, LV, S5, SV, G5, GV, P5, PV, s5t, svt, T5, TV, R5, RV2, WT, QT, QV, FT, FV,
+    rw5, rwv, rl5, rlv, pair, sent, c5, cv, csent, asem, asent, z5, zv, zsent, lsem, rq, rsent,
 ):
     s = lax.axis_index("section")
     d = lax.axis_index("dp")
@@ -72,6 +78,7 @@
     first = s == SECTIONS - 1
     lower = s > 0
     early = s < EARLY
+    eager = s < EAGER
     u = lax.rem(d, HALF)
 
     barrier = pltpu.get_barrier_semaphore()
@@ -93,7 +100,17 @@
         pl.semaphore_signal(barrier, inc=1, device_id=(s + 1, d), device_id_type=MESH)
 
     W5[:, ds(d * RT, RT, RT)] = w5[...].T
-    sections = lax.div(s + SECTIONS - 1, SECTIONS) + lax.div(2 * SECTIONS - 2 - s, SECTIONS)
+    @pl.when(s < RELAYED)
+    def _():
+        pl.semaphore_signal(barrier, inc=1, device_id=(s + RELAY, d), device_id_type=MESH)
+
+    @pl.when(jnp.logical_and(s >= RELAY, s < RELAY + RELAYED))
+    def _():
+        pl.semaphore_signal(barrier, inc=1, device_id=(s - RELAY, d), device_id_type=MESH)
+
+    helps = jnp.logical_or(s < RELAYED, jnp.logical_and(s >= RELAY, s < RELAY + RELAYED))
+    sections = helps.astype(jnp.int32)
+    sections += lax.div(s + SECTIONS - 1, SECTIONS) + lax.div(2 * SECTIONS - 2 - s, SECTIONS)
     pl.semaphore_wait(barrier, DP - 1 + sections)
 
     gw5 = Gather(
@@ -279,6 +296,10 @@
 
             own(gl5, k)
 
+            @pl.when(eager)
+            def _():
+                forward_when(gl5, 0, 1, k - LAG)
+
             @pl.when(jnp.logical_not(early))
             def _():
                 for i, (h, r) in enumerate(image_steps):
@@ -317,12 +338,36 @@
             device_id=(s, zp), device_id_type=MESH,
         )
 
+    def away(stage, kind, i):
+        width = (CT, 256)[kind]
+        here, there = pl.ds(i * width, width), pl.ds((i + KEPT[kind]) * width, width)
+        out, first_stop, second_stop, got = ((T5, QT, FT, R5), (TV, QV, FV, RV2))[kind]
+        src = (out.at[:, there], first_stop.at[:, here], second_stop.at[:, here])[stage]
+        dst = (first_stop.at[:, here], second_stop.at[:, here], got.at[:, there])[stage]
+        recv = rq.at[stage, kind, i] if stage < 2 else (z5, zv)[kind].at[i + KEPT[kind]]
+        to = ((s + RELAY, d), (s, zp), (s - RELAY, d))[stage]
+        return pltpu.make_async_remote_copy(
+            src_ref=src, dst_ref=dst, send_sem=zsent.at[kind] if stage == 0 else rsent.at[stage - 1, kind, i],
+            recv_sem=recv, device_id=to, device_id_type=MESH,
+        )
+
     def far_rows(saved, local, rows, out, got, recv, sem, width):
         def one(n, _):
             cols = ds(n * width, width, width)
             term = nn(saved[pl.ds(rows, rows), :], local[:, cols]) * (1.0 / TOK)
             out[:, cols] = term.astype(jnp.bfloat16)
-            exchange(out, got, recv, sem, n, width).start()
+            far = jnp.logical_and(s < RELAYED, n >= KEPT[sem])
+
+            @pl.when(jnp.logical_not(far))
+            def _():
+                exchange(out, got, recv, sem, n, width).start()
+
+            for i in range(2):
+
+                @pl.when(jnp.logical_and(far, n == i + KEPT[sem]))
+                def _():
+                    away(0, sem, i).start()
+
             return 0
 
         lax.fori_loop(0, local.shape[1] // width, one, 0)
@@ -360,7 +405,18 @@
         def _():
             image_hop(k).start()
 
-        forward(gl5, 0, 1, k)
+
+        @pl.when(jnp.logical_or(jnp.logical_not(eager), k < LAG))
+        def _():
+            forward(gl5, 0, 1, k + jnp.where(eager, MB - LAG, 0))
+
+        @pl.when(eager)
+        def _():
+            forward(gl5, 0, 2, k)
+
+            @pl.when(lax.rem(k, MB // CHUNKS_V) == MB // CHUNKS_V - 1)
+            def _():
+                own(glv, lax.div(k, MB // CHUNKS_V))
 
         return 0
 
@@ -372,8 +428,11 @@
 
         lax.fori_loop(0, g.pieces, one, 0)
 
-    ring_phase(gl5, 2)
-    own_all(glv)
+    @pl.when(jnp.logical_not(eager))
+    def _():
+        ring_phase(gl5, 2)
+        own_all(glv)
+
     ring_phase(gl5, 3)
     pair_done(gl5)
     saved_done(S5, 0)
@@ -388,6 +447,20 @@
     near_rows(SV, LV, RV, dvo, 256)
     add_far(d5o, T5, R5, z5, 0, CT)
     add_far(dvo, TV, RV2, zv, 1, 256)
+    @pl.when(jnp.logical_and(s >= RELAY, s < RELAY + RELAYED))
+    def _():
+        for kind in range(2):
+            for i in range(2):
+                away(0, kind, i).wait_recv()
+                away(1, kind, i).start()
+            for i in range(2):
+                away(1, kind, i).wait_recv()
+                away(2, kind, i).start()
+        for kind in range(2):
+            for i in range(2):
+                away(1, kind, i).wait_send()
+                away(2, kind, i).wait_send()
+
     for g in (gw5, gwv, gl5, glv):
         sent_done(g)
     for i, (ref, size) in enumerate(((s5t, RT), (svt, RV))):
@@ -433,6 +506,10 @@
             pltpu.VMEM((RT, DT), bf),
             pltpu.VMEM((RV, DV), bf),
             pltpu.VMEM((DV, DV), bf),
+            pltpu.VMEM((RT, 2 * CT), bf),
+            pltpu.VMEM((RV, 512), bf),
+            pltpu.VMEM((RT, 2 * CT), bf),
+            pltpu.VMEM((RV, 512), bf),
             dma((2, 4, PARTS)),
             dma((2, 4, 1)),
             dma((1, 4, CHUNKS)),
@@ -448,6 +525,8 @@
             dma((DV // 256,)),
             dma((2,)),
             dma((4,)),
+            dma((2, 2, 2)),
+            dma((2, 2, 2)),
         ],
         compiler_params=pltpu.CompilerParams(
             collective_id=0, has_side_effects=True, vmem_limit_bytes=60 * 1024 * 1024

time: 198 us -> 195 us (0.985)
  Pallas kernels: 193 us -> 190 us
    pallas_call x1, Pallas kernels: 193 us -> 190 us  [shards(): pl.pallas_call(kernel, out_shape=(jax.ShapeDtypeStruct((TOK, DT), bf), ja...]
where the time goes in v4:
time: 195 us
  Pallas kernels  190 us (97%)
  local copies, waits for them, and re-layouts  4.32 us (2%)
    pallas_call x1, Pallas kernels, shards(): pl.pallas_call(kernel, out_shape=(jax.ShapeDtypeStruct((TOK, DT), bf), ja...  190 us
    unnamed x10, local copies, waits for them, and re-layouts  4.32 us

profile of v4, /device:TPU:1, one launch (start us, length us, event | category | flops | bytes accessed | tf_op | source)
XLA Modules:
  0.0 194.9 jit_solution(15607475513516918310)
XLA Ops:
  0.6 189.9 %branches.1 = (bf16[128,2048]{1,0:T(8,128)(2,1)}, bf16[128,1280]{1,0:T(8,128)(2,1)}, f32[128,2048]{1,0:T(8,128)}, f32[80,1280]{1,0:T(8,128)}) custom-call(bf16[128,2048]{1,0:T(8,128)(2,1)} %bitcast.11, bf16[80,1280]{1,0:T(8,128)(2,1)} %bitcast.19, bf16[128,2048]{1,0:T(8,128)(2,1)} %bitcast.12, bf16[128,1280]{1,0:T(8,128)(2,1)} %bitcast.16, ...), custom_call_target="tpu_custom_call" | custom-call | tf_op jit(solution)/shard_map/branches/pallas_call | solution.py:481
  190.6 0.0 copy-start.1
  190.6 0.0 copy-start.2
  190.6 1.8 copy.14
  192.4 0.0 copy-done.1
  192.4 0.0 copy-start
  192.4 0.8 copy.15
  193.2 0.0 copy-done.2
  193.2 0.8 copy.16
  193.9 0.0 copy-done
  193.9 1.0 copy.17
Async XLA Ops:
  190.6 1.8 copy-start.1
  190.6 2.6 %copy-start.2 = (f32[80,1280]{1,0:T(8,128)S(1)}, f32[80,1280]{1,0:T(8,128)}, u32[]{:S(2)}) copy-start(f32[80,1280]{1,0:T(8,128)} %get-tuple-element.10) | copy-start | bytes 1228804
  192.4 1.6 copy-start

commit v5 on v4

--- a/solution.py
+++ b/solution.py
@@ -57,10 +57,11 @@
 
 
 def kernel(
-    w5, wv, s5, sv, top5, topv,
-    g5o, gvo, d5o, dvo,
+    w5, wv, s5_hbm, sv_hbm, top5, topv,
+    g5_hbm, gv_hbm, d5_hbm, dv_hbm,
     W5, WV, L5, LV, S5, SV, G5, GV, P5, PV, s5t, svt, T5, TV, R5, RV2, WT, QT, QV, FT, FV,
     rw5, rwv, rl5, rlv, pair, sent, c5, cv, csent, asem, asent, z5, zv, zsent, lsem, rq, rsent,
+    g5o, gvo, d5o, dvo, s5, sv, isem, osem,
 ):
     s = lax.axis_index("section")
     d = lax.axis_index("dp")
@@ -81,6 +82,9 @@
     eager = s < EAGER
     u = lax.rem(d, HALF)
 
+    reads = [pltpu.make_async_copy(a, b, isem.at[i]) for i, (a, b) in enumerate(((s5_hbm, s5), (sv_hbm, sv)))]
+    for copy in reads:
+        copy.start()
     barrier = pltpu.get_barrier_semaphore()
 
     def greet(p, _):
@@ -197,6 +201,8 @@
         own(gw5, q)
     own_wv.wait()
     own_far(gwv, 0)
+    for copy in reads:
+        copy.wait()
     s5t[...] = s5[...].T
     svt[...] = sv[...].T
 
@@ -380,11 +386,16 @@
 
         lax.fori_loop(0, local.shape[1] // width, one, 0)
 
-    def add_far(total, out, got, recv, sem, width):
+    def put(total, n, width, hbm, sem):
+        cols = ds(n * width, width, width)
+        return pltpu.make_async_copy(total.at[:, cols], hbm.at[:, cols], osem.at[sem])
+
+    def add_far(total, out, got, recv, sem, width, hbm):
         def one(n, _):
             cols = ds(n * width, width, width)
             exchange(out, got, recv, sem, n, width).wait_recv()
             total[:, cols] += got[:, cols].astype(jnp.float32)
+            put(total, n, width, hbm, sem).start()
             return 0
 
         lax.fori_loop(0, total.shape[1] // width, one, 0)
@@ -421,6 +432,9 @@
         return 0
 
     lax.fori_loop(0, MB, image_tick, 0)
+    writes = [pltpu.make_async_copy(a, b, osem.at[2 + i]) for i, (a, b) in enumerate(((g5o, g5_hbm), (gvo, gv_hbm)))]
+    for copy in writes:
+        copy.start()
     def own_all(g):
         def one(q, _):
             own(g, q)
@@ -445,8 +459,8 @@
     saved_done(SV, 1)
     far_rows(SV, LV, RV, TV, RV2, zv, 1, 256)
     near_rows(SV, LV, RV, dvo, 256)
-    add_far(d5o, T5, R5, z5, 0, CT)
-    add_far(dvo, TV, RV2, zv, 1, 256)
+    add_far(d5o, T5, R5, z5, 0, CT, d5_hbm)
+    add_far(dvo, TV, RV2, zv, 1, 256, dv_hbm)
     @pl.when(jnp.logical_and(s >= RELAY, s < RELAY + RELAYED))
     def _():
         for kind in range(2):
@@ -463,6 +477,10 @@
 
     for g in (gw5, gwv, gl5, glv):
         sent_done(g)
+    for copy in writes:
+        copy.wait()
+    pltpu.make_async_copy(d5o, d5_hbm, osem.at[0]).wait()
+    pltpu.make_async_copy(dvo, dv_hbm, osem.at[1]).wait()
     for i, (ref, size) in enumerate(((s5t, RT), (svt, RV))):
         gone = ref.at[pl.ds(0, 2 * (HALF - 1) * size), :]
         pltpu.make_async_copy(gone, gone, asent.at[i]).wait()
@@ -475,9 +493,23 @@
         pltpu.make_async_copy(gvo, gvo, csent.at[1]).wait()
 
 
+def hand_over(*refs):
+    given, out, held, came, went = refs[:4], refs[4:8], refs[8:12], refs[12], refs[13]
+    reads = [pltpu.make_async_copy(a, b, came.at[i]) for i, (a, b) in enumerate(zip(given, held))]
+    writes = [pltpu.make_async_copy(a, b, went.at[i]) for i, (a, b) in enumerate(zip(held, out))]
+    for copy in reads:
+        copy.start()
+    for read, write in zip(reads, writes):
+        read.wait()
+        write.start()
+    for copy in writes:
+        copy.wait()
+
+
 def shards(vit_weight, t5_weight, vit_saved, t5_saved, vit_top_grad, t5_top_grad):
     bf, f32 = jnp.bfloat16, jnp.float32
     dma, vmem = pltpu.SemaphoreType.DMA, pl.BlockSpec(memory_space=pltpu.VMEM)
+    hbm = pl.BlockSpec(memory_space=pl.ANY)
     g5, gv, d5, dv = pl.pallas_call(
         kernel,
         out_shape=(
@@ -486,8 +518,8 @@
             jax.ShapeDtypeStruct((RT, DT), f32),
             jax.ShapeDtypeStruct((RV, DV), f32),
         ),
-        in_specs=[vmem] * 6,
-        out_specs=[vmem] * 4,
+        in_specs=[vmem, vmem, hbm, hbm, hbm, hbm],
+        out_specs=[hbm] * 4,
         scratch_shapes=[
             pltpu.VMEM((DT, DT), bf),
             pltpu.VMEM((DV, DV), bf),
@@ -527,6 +559,14 @@
             dma((4,)),
             dma((2, 2, 2)),
             dma((2, 2, 2)),
+            pltpu.VMEM((TOK, DT), bf),
+            pltpu.VMEM((TOK, DV), bf),
+            pltpu.VMEM((RT, DT), f32),
+            pltpu.VMEM((RV, DV), f32),
+            pltpu.VMEM((TOK, DT), bf),
+            pltpu.VMEM((TOK, DV), bf),
+            dma((2,)),
+            dma((4,)),
         ],
         compiler_params=pltpu.CompilerParams(
             collective_id=0, has_side_effects=True, vmem_limit_bytes=60 * 1024 * 1024
@@ -540,6 +580,14 @@
         t5_top_grad.reshape(TOK, DT),
         vit_top_grad.reshape(TOK, DV),
     )
+    gv, g5, dv, d5 = pl.pallas_call(
+        hand_over,
+        out_shape=tuple(jax.ShapeDtypeStruct(a.shape, a.dtype) for a in (gv, g5, dv, d5)),
+        in_specs=[hbm] * 4,
+        out_specs=[hbm] * 4,
+        scratch_shapes=[pltpu.VMEM(a.shape, a.dtype) for a in (gv, g5, dv, d5)] + [dma((4,)), dma((4,))],
+        name="hand_over",
+    )(gv, g5, dv, d5)
     return (
         gv.reshape(vit_saved.shape),
         g5.reshape(t5_saved.shape),

time: 195 us -> 192 us (0.985)
  local copies, waits for them, and re-layouts: 4.32 us -> 0 us
    unnamed x10 -> x0, local copies, waits for them, and re-layouts: 4.32 us -> none
    pallas_call x0 -> x1, Pallas kernels: none -> 2.65 us  [shards(): pl.pallas_call(hand_over, out_shape=tuple((jax.ShapeDtypeStruct(a.shape,...]
where the time goes in v5:
time: 192 us
  Pallas kernels  191 us (99%)
    pallas_call x1, Pallas kernels, shards(): pl.pallas_call(kernel, out_shape=(jax.ShapeDtypeStruct((TOK, DT), bf), ja...  189 us

profile of v5, /device:TPU:1, one launch (start us, length us, event | category | flops | bytes accessed | tf_op | source)
XLA Modules:
  0.0 191.9 jit_solution(4639912633503743402)
XLA Ops:
  0.6 188.6 %branches.1 = (bf16[128,2048]{1,0:T(8,128)(2,1)}, bf16[128,1280]{1,0:T(8,128)(2,1)}, f32[128,2048]{1,0:T(8,128)}, f32[80,1280]{1,0:T(8,128)}) custom-call(bf16[128,2048]{1,0:T(8,128)(2,1)} %bitcast.10, bf16[80,1280]{1,0:T(8,128)(2,1)} %bitcast.15, bf16[128,2048]{1,0:T(8,128)(2,1)} %bitcast.11, bf16[128,1280]{1,0:T(8,128)(2,1)} %bitcast.13, ...), custom_call_target="tpu_custom_call" | custom-call | tf_op jit(solution)/shard_map/branches/pallas_call | solution.py:513
  189.2 2.7 %hand_over.1 = (bf16[128,1280]{1,0:T(8,128)(2,1)}, bf16[128,2048]{1,0:T(8,128)(2,1)}, f32[80,1280]{1,0:T(8,128)}, f32[128,2048]{1,0:T(8,128)}) custom-call(bf16[128,1280]{1,0:T(8,128)(2,1)} %get-tuple-element.12.refs_0_, bf16[128,2048]{1,0:T(8,128)(2,1)} %get-tuple-element.13.refs_1_, f32[80,1280]{1,0:T(8,128)} %get-tuple-element.14.refs_2_, ...), custom_call_target="tpu_custom_call" | custom-call | tf_op jit(solution)/shard_map/hand_over/pallas_call | solution.py:583

commit v6 on v5

--- a/solution.py
+++ b/solution.py
@@ -165,7 +165,7 @@
         push(g, owner, q, g.recv.at[h, r, q], nx).wait_recv()
         if r < 3:
             push(g, owner, q, g.recv.at[h, r + 1, q], nx).start()
-        push(g, owner, q, g.pair, pt).start()
+        push(g, owner, q, pair.at[4] if g is gw5 and h == 1 else g.pair, pt).start()
 
     def forward_when(g, h, r, q):
         @pl.when(jnp.logical_and(q >= 0, q < g.pieces))
@@ -179,13 +179,13 @@
 
         lax.fori_loop(0, g.pieces, one, 0)
 
-    def far_phase(g):
+    def far_phase(g, begin=0, end=None):
         def one(w, _):
             for r in range(4):
                 forward_when(g, 1, r, w - r)
             return 0
 
-        lax.fori_loop(0, g.pieces + 3, one, 0)
+        lax.fori_loop(begin, g.pieces + 3 if end is None else end, one, 0)
 
     def pair_done(g):
         ref = g.part(4 * g.halves)
@@ -231,14 +231,26 @@
 
     for r in (1, 2, 3):
         ring_phase(gw5, r)
-    far_phase(gw5)
+    far_phase(gw5, 0, 1)
+    share = gw5.part(4)
+    pltpu.make_async_copy(share, share, gw5.pair).wait()
+    near = ds(zh * (DT // 2), DT // 2, DT // 2)
+    far_half = ds((1 - zh) * (DT // 2), DT // 2, DT // 2)
+
+    def text_near(j, _):
+        cols = ds(j * CT, CT, CT)
+        P5[:, cols] = nt(s5[:, near], W5[cols, near])
+        return 0
+
+    lax.fori_loop(0, DT // CT, text_near, 0)
+    far_phase(gw5, 1)
     own_ring(gwv, 0)
     own_pair(gwv, 0)
-    pair_done(gw5)
+    pltpu.make_async_copy(share, share, pair.at[4]).wait()
 
     def text_slope(j, _):
         cols = ds(j * CT, CT, CT)
-        P5[:, cols] = slope_of(nt(s5[...], W5[cols, :]))
+        P5[:, cols] = slope_of(P5[:, cols] + nt(s5[:, far_half], W5[cols, far_half]))
         return 0
 
     lax.fori_loop(0, DT // CT, text_slope, 0)
@@ -546,7 +558,7 @@
             dma((2, 4, 1)),
             dma((1, 4, CHUNKS)),
             dma((1, 4, CHUNKS_V)),
-            dma((4,)),
+            dma((5,)),
             dma((4,)),
             dma((MB, DT // CT)),
             dma((MB,)),

time: 192 us -> 191 us (level)
  no operation moved by 1% of the time
where the time goes in v6:
time: 191 us
  Pallas kernels  190 us (99%)
    pallas_call x1, Pallas kernels, shards(): pl.pallas_call(kernel, out_shape=(jax.ShapeDtypeStruct((TOK, DT), bf), ja...  187 us

profile of v6, /device:TPU:1, one launch (start us, length us, event | category | flops | bytes accessed | tf_op | source)
XLA Modules:
  0.0 190.6 jit_solution(857869809480013044)
XLA Ops:
  0.6 187.3 %branches.1 = (bf16[128,2048]{1,0:T(8,128)(2,1)}, bf16[128,1280]{1,0:T(8,128)(2,1)}, f32[128,2048]{1,0:T(8,128)}, f32[80,1280]{1,0:T(8,128)}) custom-call(bf16[128,2048]{1,0:T(8,128)(2,1)} %bitcast.10, bf16[80,1280]{1,0:T(8,128)(2,1)} %bitcast.15, bf16[128,2048]{1,0:T(8,128)(2,1)} %bitcast.11, bf16[128,1280]{1,0:T(8,128)(2,1)} %bitcast.13, ...), custom_call_target="tpu_custom_call" | custom-call | tf_op jit(solution)/shard_map/branches/pallas_call | solution.py:525
  187.9 2.7 %hand_over.1 = (bf16[128,1280]{1,0:T(8,128)(2,1)}, bf16[128,2048]{1,0:T(8,128)(2,1)}, f32[80,1280]{1,0:T(8,128)}, f32[128,2048]{1,0:T(8,128)}) custom-call(bf16[128,1280]{1,0:T(8,128)(2,1)} %get-tuple-element.12.refs_0_, bf16[128,2048]{1,0:T(8,128)(2,1)} %get-tuple-element.13.refs_1_, f32[80,1280]{1,0:T(8,128)} %get-tuple-element.14.refs_2_, ...), custom_call_target="tpu_custom_call" | custom-call | tf_op jit(solution)/shard_map/hand_over/pallas_call | solution.py:595
